TPU v7x, 32 devices: a whole 2x2x4 slice. The times are simulated.
32 devices in a mesh: head: 4 (over x, core), inner: 2 (over y), outer: 4 (over z).
Axes of the slice: x: 2, y: 2, z: 4, core: 2. Of those that a mesh axis runs over, the one named last changes fastest.
Arguments:
- rotated_asking_matrix: bfloat16 [4096, 32, 128], P(('head', 'inner', 'outer')), may hold values from -12 to 12
- rotated_lookup_matrix: bfloat16 [4096, 8, 128], P(('head', 'inner', 'outer')), may hold values from -6 to 6
- content_matrix: bfloat16 [4096, 8, 128], P(('head', 'inner', 'outer')), may hold values from -6 to 6
Outputs:
- attended: bfloat16 [4096, 32, 128], P(('head', 'inner', 'outer'))
All inputs are finite; a program needn't handle non-finite values.
Results may differ from a plain program's by a relative error of at most 0.001.
Values may be sent and summed in bfloat16 or wider, within the bound.
A program may use at most 64 MiB of HBM per device.

v0:
```python
import math
import jax
import jax.numpy as jnp
from jax import lax
from jax.sharding import PartitionSpec as P


def for_sending(x):

    def short(part):
        return part.astype(jnp.bfloat16) if part.dtype == jnp.float32 else part

    return jax.tree.map(short, x)


def passed_along(x, axis, by):
    size = lax.axis_size(axis)
    return lax.ppermute(x, axis, [(i, (i + by) % size) for i in range(size)])


def shards(rotated_asking_matrix, rotated_lookup_matrix, content_matrix):
    query_local, key_local, value_local = (
        lax.all_to_all(rotated_asking_matrix, "head", split_axis=1, concat_axis=0, tiled=True),
        lax.all_to_all(rotated_lookup_matrix, "head", split_axis=1, concat_axis=0, tiled=True),
        lax.all_to_all(content_matrix, "head", split_axis=1, concat_axis=0, tiled=True),
    )
    inner_count = lax.axis_size("inner")
    outer_count = lax.axis_size("outer")
    cycle_count = inner_count * outer_count
    block_len = rotated_asking_matrix.shape[0]
    local_len = key_local.shape[0]
    kv_heads = key_local.shape[1]
    group_size = query_local.shape[1] // kv_heads
    head_dim = query_local.shape[2]
    grouped = query_local.reshape(local_len, kv_heads, group_size, head_dim)
    inner_self = lax.axis_index("inner")
    outer_self = lax.axis_index("outer")
    offsets = jnp.arange(local_len, dtype=jnp.int32)
    score_scale = 1.0 / math.sqrt(head_dim)

    def places(cycle_id):
        return (offsets // block_len * cycle_count + cycle_id) * block_len + offsets % block_len

    query_pos = places(inner_self * outer_count + outer_self)

    def absorb(carry, key_block, value_block, key_pos):
        run_max, run_sum, accum = carry
        scores = (
            jnp.einsum("tkgd,skd->kgts", grouped, key_block, preferred_element_type=jnp.float32)
            * score_scale
        )
        allowed = key_pos[None, :] <= query_pos[:, None]
        scores = jnp.where(allowed, scores, -1e30)
        new_max = jnp.maximum(run_max, jnp.max(scores, axis=-1))
        factor = jnp.exp(run_max - new_max)
        weights = jnp.where(allowed, jnp.exp(scores - new_max[..., None]), 0.0)
        run_sum = run_sum * factor + jnp.sum(weights, axis=-1)
        mixed = jnp.einsum(
            "kgts,skd->kgtd",
            weights,
            value_block.astype(jnp.float32),
            precision=lax.Precision.HIGHEST,
        )
        accum = accum * factor[..., None] + mixed
        return (new_max, run_sum, accum)

    def sweep(carry, window, outer_step):
        outer_source = (outer_self - outer_step) % outer_count

        def cycle_pos(inner_source):
            return places(inner_source * outer_count + outer_source)

        carry = absorb(carry, window[0], window[1], cycle_pos(inner_self))

        def inner_body(inner_step, loop_state):
            carry_state, moving = loop_state
            moving = jax.tree.map(
                lambda part, own: part.astype(own.dtype),
                passed_along(for_sending(moving), "inner", 1),
                moving,
            )
            key_pos = cycle_pos((inner_self - inner_step) % inner_count)
            carry_state = absorb(carry_state, moving[0], moving[1], key_pos)
            return (carry_state, moving)

        carry, moving = lax.fori_loop(1, inner_count, inner_body, (carry, window))
        return carry

    carry = (
        jnp.full((kv_heads, group_size, local_len), -1e30, jnp.float32),
        jnp.zeros((kv_heads, group_size, local_len), jnp.float32),
        jnp.zeros((kv_heads, group_size, local_len, head_dim), jnp.float32),
    )
    window = jnp.stack([key_local, value_local])

    def outer_body(outer_step, loop_state):
        carry_state, current = loop_state
        upcoming = jax.tree.map(
            lambda part, own: part.astype(own.dtype),
            passed_along(for_sending(current), "outer", 1),
            current,
        )
        carry_state = sweep(carry_state, current, outer_step)
        return (carry_state, upcoming)

    carry, window = lax.fori_loop(0, outer_count - 1, outer_body, (carry, window))
    carry = sweep(carry, window, outer_count - 1)
    run_max, run_sum, accum = carry
    result = (accum / run_sum[..., None]).astype(jnp.bfloat16)
    result = result.transpose(2, 0, 1, 3).reshape(local_len, kv_heads * group_size, head_dim)
    return lax.all_to_all(result, "head", split_axis=0, concat_axis=1, tiled=True)


def solution(mesh):
    placed = (
        P(("head", "inner", "outer"), None, None),
        P(("head", "inner", "outer"), None, None),
        P(("head", "inner", "outer"), None, None),
    )
    return jax.shard_map(
        shards,
        mesh=mesh,
        in_specs=placed,
        out_specs=P(("head", "inner", "outer"), None, None),
        check_vma=False,
    )
```

profile of v0, /device:TPU:0, one launch (start us, length us, event | category | flops | bytes accessed | tf_op | source)
XLA Modules:
  0.0 204.6 jit_solution(4616779751320213047)
XLA Ops:
  0.0 1.7 copy.14
  1.7 4.2 %all-to-all-start = ((bf16[128,8,128]{2,0,1:T(8,128)(2,1)}), bf16[128,8,128]{2,0,1:T(8,128)(2,1)S(1)}, u32[]{:S(2)}, u32[]{:S(2)}) async-start(bf16[128,8,128]{2,0,1:T(8,128)(2,1)} %copy.14), calls=%async_computation | async-start | bytes 524288 | tf_op jit(solution)/shard_map/all_to_all | solution.py:24
  5.9 1.7 copy.16
  7.6 4.3 %all-to-all-done = bf16[128,8,128]{2,0,1:T(8,128)(2,1)S(1)} async-done(((bf16[128,8,128]{2,0,1:T(8,128)(2,1)}), bf16[128,8,128]{2,0,1:T(8,128)(2,1)S(1)}, u32[]{:S(2)}, u32[]{:S(2)}) %all-to-all-start) | async-done | bytes 262176 | tf_op jit(solution)/shard_map/all_to_all | solution.py:24
  11.9 3.4 %all-to-all-start.1 = ((bf16[128,8,128]{2,0,1:T(8,128)(2,1)}), bf16[128,8,128]{2,0,1:T(8,128)(2,1)S(1)}, u32[]{:S(2)}, u32[]{:S(2)}) async-start(bf16[128,8,128]{2,0,1:T(8,128)(2,1)} %copy.16), calls=%async_computation.1 | async-start | bytes 524288 | tf_op jit(solution)/shard_map/all_to_all | solution.py:25
  15.3 2.6 %copy.18 = bf16[128,32,128]{2,0,1:T(8,128)(2,1)} copy(bf16[128,32,128]{2,1,0:T(8,128)(2,1)} %param.5) | data formatting | bytes 2097152 | tf_op args[0]
  17.9 3.4 %all-to-all-done.1 = bf16[128,8,128]{2,0,1:T(8,128)(2,1)S(1)} async-done(((bf16[128,8,128]{2,0,1:T(8,128)(2,1)}), bf16[128,8,128]{2,0,1:T(8,128)(2,1)S(1)}, u32[]{:S(2)}, u32[]{:S(2)}) %all-to-all-start.1) | async-done | bytes 262176 | tf_op jit(solution)/shard_map/all_to_all | solution.py:25
  21.3 3.5 %all-to-all-start.2 = ((bf16[128,32,128]{2,0,1:T(8,128)(2,1)}), bf16[128,32,128]{2,0,1:T(8,128)(2,1)S(1)}, u32[]{:S(2)}, u32[]{:S(2)}) async-start(bf16[128,32,128]{2,0,1:T(8,128)(2,1)} %copy.18), calls=%async_computation.2 | async-start | bytes 2097152 | tf_op jit(solution)/shard_map/all_to_all | solution.py:23
  25.1 14.2 %all-to-all-done.2 = bf16[128,32,128]{2,0,1:T(8,128)(2,1)S(1)} async-done(((bf16[128,32,128]{2,0,1:T(8,128)(2,1)}), bf16[128,32,128]{2,0,1:T(8,128)(2,1)S(1)}, u32[]{:S(2)}, u32[]{:S(2)}) %all-to-all-start.2) | async-done | bytes 1048608 | tf_op jit(solution)/shard_map/all_to_all | solution.py:23
  39.3 111.7 %while.49 = (s32[]{:T(128)}, f32[2,4,512]{2,1,0:T(4,128)S(1)}, f32[2,4,512]{2,1,0:T(4,128)S(1)}, f32[2,4,512,128]{3,2,1,0:T(8,128)}, bf16[2,512,2,128]{3,1,2,0:T...) while((s32[]{:T(128)}, f32[2,4,512]{2,1,0:T(4,128)S(1)}, ...), condition=%wide.region_5.6_spmd.clone.clone, body=%wide.region_0.5_spmd.clone.clone.sunk | while | flops 7569716736 | bytes 86422968 | solution.py:106
  39.4 2.2 %collective-permute-start = (bf16[2,512,2,128]{3,1,2,0:T(8,128)(2,1)S(1)}, bf16[2,512,2,128]{3,1,2,0:T(8,128)(2,1)S(1)}, u32[]{:S(2)}, u32[]{:S(2)}) collective-permute-start(bf16[2,512,2,128]{3,1,2,0:T(8,128)(2,1)S(1)} %copy.47), channel_id=1, source_target_pairs={{0,4},{4,0},{1,5},{5,1},{2,6},{6,2},{3,7},{7,3},{8,12},{12,8},{9,1... | collective-permute-start | bytes 1572872 | tf_op jit(solution)/shard_map/while/body/eval_jaxpr/while/body/eval_jaxpr/ppermute | solution.py:18
  41.6 1.6 collective-permute-start.1
  43.3 0.4 broadcast_compare_fusion.5
  43.6 1.5 fusion.113
  45.2 8.1 %collective-permute-done = bf16[2,512,2,128]{3,1,2,0:T(8,128)(2,1)S(1)} collective-permute-done((bf16[2,512,2,128]{3,1,2,0:T(8,128)(2,1)S(1)}, bf16[2,512,2,128]{3,1,2,0:T(8,128)(2,1)S(1)}, u32[]{:S(2)}, u32[]{:S(2)}) %collective-permute-start) | collective-permute-done | bytes 524320 | tf_op jit(solution)/shard_map/while/body/eval_jaxpr/while/body/eval_jaxpr/ppermute | solution.py:18
  53.2 1.5 fusion.112
  54.8 7.6 %fusion.117 = f32[2,4,512,128]{3,2,1,0:T(8,128)S(1)} fusion(f32[2,512,512,4]{2,1,3,0:T(8,128)S(1)} %get-tuple-element.740, f32[2,4,512]{2,1,0:T(4,128)S(1)} %get-tuple-element.741, pred[512,512]{0,1:T(8,128)(4,1)S(1)} %get-tuple-element.737, bf16[2,512,2,128]{3,1,2,0:T(8,128)(2,1)S(1)} %copy.47), kind=kOutput, calls=%fused_computation.11.clone.1 | convolution fusion | flops 3229614080 | bytes 11026432 | tf_op jit(solution)/shard_map/while/body/eval_jaxpr/kgts,skd->kgtd/dot_general | solution.py:58
  62.4 4.1 %fusion.115 = (f32[2,4,512]{2,1,0:T(4,128)S(1)}, f32[2,4,512]{2,1,0:T(4,128)S(1)}) fusion(f32[2,512,512,4]{2,1,3,0:T(8,128)S(1)} %get-tuple-element.740, f32[2,4,512]{2,1,0:T(4,128)S(1)} %get-tuple-element.741, pred[512,512]{0,1:T(8,128)(4,1)S(1)} %get-tuple-element.737, f32[2,4,512]{2,1,0:T(4,128)S(1)} %get-tuple-element.777, ...), kind=kLoop, calls=%fused_computation.12.clone.1 | loop fusion | flops 20963328 | bytes 17367040 | tf_op jit(solution)/shard_map/while/body/eval_jaxpr/reduce_sum | solution.py:57
  66.5 9.6 %fusion.118 = f32[2,4,512,128]{3,2,1,0:T(8,128)S(1)} fusion(f32[2,4,512,128]{3,2,1,0:T(8,128)S(1)} %fusion.117, f32[2,4,512,128]{3,2,1,0:T(8,128)S(1)} %copy-done, f32[2,512,512,4]{2,1,3,0:T(8,128)S(1)} %get-tuple-element.742, f32[2,4,512]{2,1,0:T(4,128)S(1)} %get-tuple-element.777, pred[512,512]{0,1:T(8,128)(4,1)S(1)} %get-tuple-element.735, ...), kind=kOutput, calls=%fused_computation.28.clone.1 | convolution fusion | flops 3232235520 | bytes 15253505 | tf_op jit(solution)/shard_map/while/body/eval_jaxpr/while/body/eval_jaxpr/kgts,skd->kgtd/dot_general | solution.py:58
  76.2 1.3 copy-done.1
  77.5 1.8 collective-permute-start
  79.3 1.6 collective-permute-start.1
  81.4 1.5 fusion.113
  82.9 7.5 %collective-permute-done = bf16[2,512,2,128]{3,1,2,0:T(8,128)(2,1)S(1)} collective-permute-done((bf16[2,512,2,128]{3,1,2,0:T(8,128)(2,1)S(1)}, bf16[2,512,2,128]{3,1,2,0:T(8,128)(2,1)S(1)}, u32[]{:S(2)}, u32[]{:S(2)}) %collective-permute-start) | collective-permute-done | bytes 524320 | tf_op jit(solution)/shard_map/while/body/eval_jaxpr/while/body/eval_jaxpr/ppermute | solution.py:18
  90.4 1.5 fusion.112
  92.0 7.6 %fusion.117 = f32[2,4,512,128]{3,2,1,0:T(8,128)S(1)} fusion(f32[2,512,512,4]{2,1,3,0:T(8,128)S(1)} %get-tuple-element.740, f32[2,4,512]{2,1,0:T(4,128)S(1)} %get-tuple-element.741, pred[512,512]{0,1:T(8,128)(4,1)S(1)} %get-tuple-element.737, bf16[2,512,2,128]{3,1,2,0:T(8,128)(2,1)S(1)} %copy.47), kind=kOutput, calls=%fused_computation.11.clone.1 | convolution fusion | flops 3229614080 | bytes 11026432 | tf_op jit(solution)/shard_map/while/body/eval_jaxpr/kgts,skd->kgtd/dot_general | solution.py:58
  99.6 4.1 %fusion.115 = (f32[2,4,512]{2,1,0:T(4,128)S(1)}, f32[2,4,512]{2,1,0:T(4,128)S(1)}) fusion(f32[2,512,512,4]{2,1,3,0:T(8,128)S(1)} %get-tuple-element.740, f32[2,4,512]{2,1,0:T(4,128)S(1)} %get-tuple-element.741, pred[512,512]{0,1:T(8,128)(4,1)S(1)} %get-tuple-element.737, f32[2,4,512]{2,1,0:T(4,128)S(1)} %get-tuple-element.777, ...), kind=kLoop, calls=%fused_computation.12.clone.1 | loop fusion | flops 20963328 | bytes 17367040 | tf_op jit(solution)/shard_map/while/body/eval_jaxpr/reduce_sum | solution.py:57
  103.7 9.6 %fusion.118 = f32[2,4,512,128]{3,2,1,0:T(8,128)S(1)} fusion(f32[2,4,512,128]{3,2,1,0:T(8,128)S(1)} %fusion.117, f32[2,4,512,128]{3,2,1,0:T(8,128)S(1)} %copy-done, f32[2,512,512,4]{2,1,3,0:T(8,128)S(1)} %get-tuple-element.742, f32[2,4,512]{2,1,0:T(4,128)S(1)} %get-tuple-element.777, pred[512,512]{0,1:T(8,128)(4,1)S(1)} %get-tuple-element.735, ...), kind=kOutput, calls=%fused_computation.28.clone.1 | convolution fusion | flops 3232235520 | bytes 15253505 | tf_op jit(solution)/shard_map/while/body/eval_jaxpr/while/body/eval_jaxpr/kgts,skd->kgtd/dot_general | solution.py:58
  113.3 1.3 copy-done.1
  114.7 1.5 collective-permute-start
  116.2 1.6 collective-permute-start.1
  118.2 1.5 fusion.113
  119.8 6.9 %collective-permute-done = bf16[2,512,2,128]{3,1,2,0:T(8,128)(2,1)S(1)} collective-permute-done((bf16[2,512,2,128]{3,1,2,0:T(8,128)(2,1)S(1)}, bf16[2,512,2,128]{3,1,2,0:T(8,128)(2,1)S(1)}, u32[]{:S(2)}, u32[]{:S(2)}) %collective-permute-start) | collective-permute-done | bytes 524320 | tf_op jit(solution)/shard_map/while/body/eval_jaxpr/while/body/eval_jaxpr/ppermute | solution.py:18
  126.7 1.5 fusion.112
  128.2 7.6 %fusion.117 = f32[2,4,512,128]{3,2,1,0:T(8,128)S(1)} fusion(f32[2,512,512,4]{2,1,3,0:T(8,128)S(1)} %get-tuple-element.740, f32[2,4,512]{2,1,0:T(4,128)S(1)} %get-tuple-element.741, pred[512,512]{0,1:T(8,128)(4,1)S(1)} %get-tuple-element.737, bf16[2,512,2,128]{3,1,2,0:T(8,128)(2,1)S(1)} %copy.47), kind=kOutput, calls=%fused_computation.11.clone.1 | convolution fusion | flops 3229614080 | bytes 11026432 | tf_op jit(solution)/shard_map/while/body/eval_jaxpr/kgts,skd->kgtd/dot_general | solution.py:58
  135.9 4.1 %fusion.115 = (f32[2,4,512]{2,1,0:T(4,128)S(1)}, f32[2,4,512]{2,1,0:T(4,128)S(1)}) fusion(f32[2,512,512,4]{2,1,3,0:T(8,128)S(1)} %get-tuple-element.740, f32[2,4,512]{2,1,0:T(4,128)S(1)} %get-tuple-element.741, pred[512,512]{0,1:T(8,128)(4,1)S(1)} %get-tuple-element.737, f32[2,4,512]{2,1,0:T(4,128)S(1)} %get-tuple-element.777, ...), kind=kLoop, calls=%fused_computation.12.clone.1 | loop fusion | flops 20963328 | bytes 17367040 | tf_op jit(solution)/shard_map/while/body/eval_jaxpr/reduce_sum | solution.py:57
  140.0 9.6 %fusion.118 = f32[2,4,512,128]{3,2,1,0:T(8,128)S(1)} fusion(f32[2,4,512,128]{3,2,1,0:T(8,128)S(1)} %fusion.117, f32[2,4,512,128]{3,2,1,0:T(8,128)S(1)} %copy-done, f32[2,512,512,4]{2,1,3,0:T(8,128)S(1)} %get-tuple-element.742, f32[2,4,512]{2,1,0:T(4,128)S(1)} %get-tuple-element.777, pred[512,512]{0,1:T(8,128)(4,1)S(1)} %get-tuple-element.735, ...), kind=kOutput, calls=%fused_computation.28.clone.1 | convolution fusion | flops 3232235520 | bytes 15253505 | tf_op jit(solution)/shard_map/while/body/eval_jaxpr/while/body/eval_jaxpr/kgts,skd->kgtd/dot_general | solution.py:58
  149.6 1.3 copy-done.1
  151.1 1.2 collective-permute-start.2
  152.7 1.5 fusion.55
  154.2 8.0 %collective-permute-done.2 = bf16[2,512,2,128]{3,1,2,0:T(8,128)(2,1)S(1)} collective-permute-done((bf16[2,512,2,128]{3,1,2,0:T(8,128)(2,1)S(1)}, bf16[2,512,2,128]{3,1,2,0:T(8,128)(2,1)S(1)}, u32[]{:S(2)}, u32[]{:S(2)}) %collective-permute-start.2) | collective-permute-done | bytes 524320 | tf_op jit(solution)/shard_map/while/body/eval_jaxpr/ppermute | solution.py:18
  162.2 1.5 fusion.56
  163.8 7.6 %fusion.58 = f32[2,4,512,128]{3,2,1,0:T(8,128)S(1)} fusion(f32[2,512,512,4]{2,1,3,0:T(8,128)S(1)} %get-tuple-element.649, f32[2,4,512]{2,1,0:T(4,128)S(1)} %bitcast.171, pred[512,512]{0,1:T(8,128)(4,1)S(1)} %get-tuple-element.644, bf16[2,512,2,128]{3,1,2,0:T(8,128)(2,1)S(1)} %get-tuple-element.515), kind=kOutput, calls=%fused_computation.78 | convolution fusion | flops 3229614080 | bytes 11026432 | tf_op jit(solution)/shard_map/kgts,skd->kgtd/dot_general | solution.py:58
  171.4 4.3 %fusion.57 = (f32[2,4,512]{2,1,0:T(4,128)S(1)}, f32[2,4,512]{2,1,0:T(4,128)S(1)}) fusion(f32[2,512,512,4]{2,1,3,0:T(8,128)S(1)} %get-tuple-element.649, f32[2,4,512]{2,1,0:T(4,128)S(1)} %bitcast.172, pred[512,512]{0,1:T(8,128)(4,1)S(1)} %get-tuple-element.644, f32[2,4,512]{2,1,0:T(4,128)S(1)} %bitcast.169, f32[2,512,512,4]{2,1,3,0:T(8,128)S(1)} %get-tuple-element.647, ...), kind=kLoop, calls=%fused_computation.77 | loop fusion | flops 20963328 | bytes 17367040 | tf_op jit(solution)/shard_map/reduce_sum | solution.py:57
  175.7 9.4 %divide_convert_fusion = bf16[2,4,512,128]{3,2,1,0:T(8,128)(2,1)S(1)} fusion(f32[2,4,512,128]{3,2,1,0:T(8,128)S(1)} %fusion.58, f32[2,4,512,128]{3,2,1,0:T(8,128)S(1)} %copy-done.2, f32[2,512,512,4]{2,1,3,0:T(8,128)S(1)} %get-tuple-element.647, f32[2,4,512]{2,1,0:T(4,128)S(1)} %bitcast.170, pred[512,512]{0,1:T(8,128)(4,1)S(1)} %get-tuple-element.645, ...), kind=kOutput, calls=%fused_computation.91 | convolution fusion | flops 3232759808 | bytes 14221312 | tf_op jit(solution)/shard_map/while/body/eval_jaxpr/kgts,skd->kgtd/dot_general | solution.py:58
  185.1 0.7 copy.22
  185.8 17.4 %all_to_all.63 = bf16[512,8,128]{2,1,0:T(8,128)(2,1)S(1)} all-to-all(bf16[512,8,128]{2,1,0:T(8,128)(2,1)S(1)} %copy.22), channel_id=1, replica_groups=mesh['head'=4,'inner'=2,'outer'=4] {'head'}, dimensions={0} | all-to-all | bytes 2097152 | tf_op jit(solution)/shard_map/all_to_all | solution.py:111
  203.1 1.1 copy.37
  (50 shorter events, 1.8 us)
Async XLA Ops:
  1.7 10.2 %all-to-all-start = ((bf16[128,8,128]{2,0,1:T(8,128)(2,1)}), bf16[128,8,128]{2,0,1:T(8,128)(2,1)S(1)}, u32[]{:S(2)}, u32[]{:S(2)}) async-start(bf16[128,8,128]{2,0,1:T(8,128)(2,1)} %copy.14), calls=%async_computation | async-start | bytes 524288 | tf_op jit(solution)/shard_map/all_to_all | solution.py:24
  11.9 9.4 %all-to-all-start.1 = ((bf16[128,8,128]{2,0,1:T(8,128)(2,1)}), bf16[128,8,128]{2,0,1:T(8,128)(2,1)S(1)}, u32[]{:S(2)}, u32[]{:S(2)}) async-start(bf16[128,8,128]{2,0,1:T(8,128)(2,1)} %copy.16), calls=%async_computation.1 | async-start | bytes 524288 | tf_op jit(solution)/shard_map/all_to_all | solution.py:25
  21.3 17.9 %all-to-all-start.2 = ((bf16[128,32,128]{2,0,1:T(8,128)(2,1)}), bf16[128,32,128]{2,0,1:T(8,128)(2,1)S(1)}, u32[]{:S(2)}, u32[]{:S(2)}) async-start(bf16[128,32,128]{2,0,1:T(8,128)(2,1)} %copy.18), calls=%async_computation.2 | async-start | bytes 2097152 | tf_op jit(solution)/shard_map/all_to_all | solution.py:23
  39.4 13.8 %collective-permute-start = (bf16[2,512,2,128]{3,1,2,0:T(8,128)(2,1)S(1)}, bf16[2,512,2,128]{3,1,2,0:T(8,128)(2,1)S(1)}, u32[]{:S(2)}, u32[]{:S(2)}) collective-permute-start(bf16[2,512,2,128]{3,1,2,0:T(8,128)(2,1)S(1)} %copy.47), channel_id=1, source_target_pairs={{0,4},{4,0},{1,5},{5,1},{2,6},{6,2},{3,7},{7,3},{8,12},{12,8},{9,1... | collective-permute-start | bytes 1572872 | tf_op jit(solution)/shard_map/while/body/eval_jaxpr/while/body/eval_jaxpr/ppermute | solution.py:18
  41.6 34.5 %collective-permute-start.1 = (bf16[2,512,2,128]{3,1,2,0:T(8,128)(2,1)S(1)}, bf16[2,512,2,128]{3,1,2,0:T(8,128)(2,1)S(1)}, u32[]{:S(2)}, u32[]{:S(2)}) collective-permute-start(bf16[2,512,2,128]{3,1,2,0:T(8,128)(2,1)S(1)} %copy.47), channel_id=1, source_target_pairs={{0,1},{1,2},{2,3},{3,0},{4,5},{5,6},{6,7},{7,4},{8,9},{9,10},{10,1... | collective-permute-start | bytes 1572872 | tf_op jit(solution)/shard_map/while/body/eval_jaxpr/ppermute | solution.py:18
  62.4 4.1 %copy-start = (f32[2,4,512,128]{3,2,1,0:T(8,128)S(1)}, f32[2,4,512,128]{3,2,1,0:T(8,128)}, u32[]{:S(2)}) copy-start(f32[2,4,512,128]{3,2,1,0:T(8,128)} %get-tuple-element.765) | copy-start | bytes 6291460 | tf_op jit(solution)/shard_map/while
  76.1 1.4 copy-start.1
  77.5 12.9 %collective-permute-start = (bf16[2,512,2,128]{3,1,2,0:T(8,128)(2,1)S(1)}, bf16[2,512,2,128]{3,1,2,0:T(8,128)(2,1)S(1)}, u32[]{:S(2)}, u32[]{:S(2)}) collective-permute-start(bf16[2,512,2,128]{3,1,2,0:T(8,128)(2,1)S(1)} %copy.47), channel_id=1, source_target_pairs={{0,4},{4,0},{1,5},{5,1},{2,6},{6,2},{3,7},{7,3},{8,12},{12,8},{9,1... | collective-permute-start | bytes 1572872 | tf_op jit(solution)/shard_map/while/body/eval_jaxpr/while/body/eval_jaxpr/ppermute | solution.py:18
  79.3 34.0 %collective-permute-start.1 = (bf16[2,512,2,128]{3,1,2,0:T(8,128)(2,1)S(1)}, bf16[2,512,2,128]{3,1,2,0:T(8,128)(2,1)S(1)}, u32[]{:S(2)}, u32[]{:S(2)}) collective-permute-start(bf16[2,512,2,128]{3,1,2,0:T(8,128)(2,1)S(1)} %copy.47), channel_id=1, source_target_pairs={{0,1},{1,2},{2,3},{3,0},{4,5},{5,6},{6,7},{7,4},{8,9},{9,10},{10,1... | collective-permute-start | bytes 1572872 | tf_op jit(solution)/shard_map/while/body/eval_jaxpr/ppermute | solution.py:18
  99.6 4.1 %copy-start = (f32[2,4,512,128]{3,2,1,0:T(8,128)S(1)}, f32[2,4,512,128]{3,2,1,0:T(8,128)}, u32[]{:S(2)}) copy-start(f32[2,4,512,128]{3,2,1,0:T(8,128)} %get-tuple-element.765) | copy-start | bytes 6291460 | tf_op jit(solution)/shard_map/while
  113.3 1.4 copy-start.1
  114.7 12.0 %collective-permute-start = (bf16[2,512,2,128]{3,1,2,0:T(8,128)(2,1)S(1)}, bf16[2,512,2,128]{3,1,2,0:T(8,128)(2,1)S(1)}, u32[]{:S(2)}, u32[]{:S(2)}) collective-permute-start(bf16[2,512,2,128]{3,1,2,0:T(8,128)(2,1)S(1)} %copy.47), channel_id=1, source_target_pairs={{0,4},{4,0},{1,5},{5,1},{2,6},{6,2},{3,7},{7,3},{8,12},{12,8},{9,1... | collective-permute-start | bytes 1572872 | tf_op jit(solution)/shard_map/while/body/eval_jaxpr/while/body/eval_jaxpr/ppermute | solution.py:18
  116.2 33.4 %collective-permute-start.1 = (bf16[2,512,2,128]{3,1,2,0:T(8,128)(2,1)S(1)}, bf16[2,512,2,128]{3,1,2,0:T(8,128)(2,1)S(1)}, u32[]{:S(2)}, u32[]{:S(2)}) collective-permute-start(bf16[2,512,2,128]{3,1,2,0:T(8,128)(2,1)S(1)} %copy.47), channel_id=1, source_target_pairs={{0,1},{1,2},{2,3},{3,0},{4,5},{5,6},{6,7},{7,4},{8,9},{9,10},{10,1... | collective-permute-start | bytes 1572872 | tf_op jit(solution)/shard_map/while/body/eval_jaxpr/ppermute | solution.py:18
  135.9 4.1 %copy-start = (f32[2,4,512,128]{3,2,1,0:T(8,128)S(1)}, f32[2,4,512,128]{3,2,1,0:T(8,128)}, u32[]{:S(2)}) copy-start(f32[2,4,512,128]{3,2,1,0:T(8,128)} %get-tuple-element.765) | copy-start | bytes 6291460 | tf_op jit(solution)/shard_map/while
  149.6 1.4 copy-start.1
  151.1 11.1 %collective-permute-start.2 = (bf16[2,512,2,128]{3,1,2,0:T(8,128)(2,1)S(1)}, bf16[2,512,2,128]{3,1,2,0:T(8,128)(2,1)S(1)}, u32[]{:S(2)}, u32[]{:S(2)}) collective-permute-start(bf16[2,512,2,128]{3,1,2,0:T(8,128)(2,1)S(1)} %get-tuple-element.515), channel_id=1, source_target_pairs={{0,4},{4,0},{1,5},{5,1},{2,6},{6,2},{3,7},{7,3},{8,12},{12,8},{9,1... | collective-permute-start | bytes 1572872 | tf_op jit(solution)/shard_map/while/body/eval_jaxpr/ppermute | solution.py:18
  171.4 4.3 %copy-start.2 = (f32[2,4,512,128]{3,2,1,0:T(8,128)S(1)}, f32[2,4,512,128]{3,2,1,0:T(8,128)}, u32[]{:S(2)}) copy-start(f32[2,4,512,128]{3,2,1,0:T(8,128)} %get-tuple-element.513) | copy-start | bytes 6291460
where the time goes:
time: 205 us
  matrix products  80.9 us (39%)
  waiting for transfers between devices  52.3 us (26%)
  starting transfers between devices  22.7 us (11%)
  other arithmetic  18.3 us (9%)
  blocking collectives  17.4 us (8%)
  local copies, waits for them, and re-layouts  12.1 us (6%)
    dot_general x8, matrix products, absorb(): jnp.einsum('kgts,skd->kgtd', weights, value_block.astype(jnp.float32), pr...  68.5 us
    ppermute x7, waiting for transfers between devices, passed_along(): return lax.ppermute(x, axis, [(i, (i + by) % size) for i in range(size)])  30.5 us
    all_to_all x1, blocking collectives, shards(): lax.all_to_all(result, 'head', split_axis=0, concat_axis=1, tiled=True)  17.4 us
    reduce_sum x4, other arithmetic, absorb(): run_sum = run_sum * factor + jnp.sum(weights, axis=-1)  16.4 us
    all_to_all x1, waiting for transfers between devices, shards(): lax.all_to_all(rotated_asking_matrix, 'head', split_axis=1, concat_axis=0...  14.2 us
    dot_general x8, matrix products, absorb(): jnp.einsum('tkgd,skd->kgts', grouped, key_block, preferred_element_type=j...  12.3 us
    ppermute x7, starting transfers between devices, passed_along(): return lax.ppermute(x, axis, [(i, (i + by) % size) for i in range(size)])  11.5 us
    unnamed x5, local copies, waits for them, and re-layouts  5.97 us
  transfers between devices with their start and end apart: 10, of which 7 were waited for; matrix products, arithmetic and copies ran while one was open for 39% of the time, Pallas kernels for 0%

commit v1 on v0

--- a/solution.py
+++ b/solution.py
@@ -20,7 +20,15 @@
 
 def shards(rotated_asking_matrix, rotated_lookup_matrix, content_matrix):
     query_local, key_local, value_local = (
-        lax.all_to_all(rotated_asking_matrix, "head", split_axis=1, concat_axis=0, tiled=True),
+        jnp.concatenate(
+            lax.all_to_all(
+                jnp.stack(jnp.split(rotated_asking_matrix, lax.axis_size("head"), axis=1)),
+                "head",
+                0,
+                0,
+            ),
+            axis=0,
+        ),
         lax.all_to_all(rotated_lookup_matrix, "head", split_axis=1, concat_axis=0, tiled=True),
         lax.all_to_all(content_matrix, "head", split_axis=1, concat_axis=0, tiled=True),
     )

time: 205 us -> 213 us (1.039)
  loops' own time: 0.47 us -> 8.34 us
    another operation x1, loops' own time: 0.47 us -> 8.34 us  [shards(): lax.fori_loop(0, outer_count - 1, outer_body, (carry, window))]
    unnamed x5 -> x4, local copies, waits for them, and re-layouts: 5.97 us -> 3.37 us
  transfers between devices with their start and end apart: 10 -> 10, of which waited for: 7 -> 7; matrix products, arithmetic and copies ran while one was open for 39% -> 38% of each run, Pallas kernels for 0% -> 0%
where the time goes in v1:
time: 213 us
  matrix products  80.9 us (38%)
  waiting for transfers between devices  52.5 us (25%)
  starting transfers between devices  22.7 us (11%)
  other arithmetic  19.4 us (9%)
  blocking collectives  17.4 us (8%)
  local copies, waits for them, and re-layouts  10.9 us (5%)
  loops' own time  8.34 us (4%)
    dot_general x8, matrix products, absorb(): jnp.einsum('kgts,skd->kgtd', weights, value_block.astype(jnp.float32), pr...  68.5 us
    ppermute x7, waiting for transfers between devices, passed_along(): return lax.ppermute(x, axis, [(i, (i + by) % size) for i in range(size)])  30.4 us
    all_to_all x1, blocking collectives, shards(): lax.all_to_all(result, 'head', split_axis=0, concat_axis=1, tiled=True)  17.4 us
    reduce_sum x4, other arithmetic, absorb(): run_sum = run_sum * factor + jnp.sum(weights, axis=-1)  16.4 us
    all_to_all x1, waiting for transfers between devices, shards(): lax.all_to_all(jnp.stack(jnp.split(rotated_asking_matrix, lax.axis_size('...  14.2 us
    dot_general x8, matrix products, absorb(): jnp.einsum('tkgd,skd->kgts', grouped, key_block, preferred_element_type=j...  12.3 us
    ppermute x7, starting transfers between devices, passed_along(): return lax.ppermute(x, axis, [(i, (i + by) % size) for i in range(size)])  11.5 us
    another operation x1, loops' own time, shards(): lax.fori_loop(0, outer_count - 1, outer_body, (carry, window))  8.34 us
  transfers between devices with their start and end apart: 10, of which 7 were waited for; matrix products, arithmetic and copies ran while one was open for 38% of the time, Pallas kernels for 0%

profile of v1, /device:TPU:0, one launch (start us, length us, event | category | flops | bytes accessed | tf_op | source)
XLA Modules:
  0.0 212.5 jit_solution(10583861661463919955)
XLA Ops:
  0.0 1.7 copy.14
  1.7 4.2 %all-to-all-start = ((bf16[128,8,128]{2,0,1:T(8,128)(2,1)}), bf16[128,8,128]{2,0,1:T(8,128)(2,1)S(1)}, u32[]{:S(2)}, u32[]{:S(2)}) async-start(bf16[128,8,128]{2,0,1:T(8,128)(2,1)} %copy.14), calls=%async_computation | async-start | bytes 524288 | tf_op jit(solution)/shard_map/all_to_all | solution.py:32
  5.9 1.7 copy.16
  7.6 4.3 %all-to-all-done = bf16[128,8,128]{2,0,1:T(8,128)(2,1)S(1)} async-done(((bf16[128,8,128]{2,0,1:T(8,128)(2,1)}), bf16[128,8,128]{2,0,1:T(8,128)(2,1)S(1)}, u32[]{:S(2)}, u32[]{:S(2)}) %all-to-all-start) | async-done | bytes 262176 | tf_op jit(solution)/shard_map/all_to_all | solution.py:32
  11.9 3.4 %all-to-all-start.1 = ((bf16[128,8,128]{2,0,1:T(8,128)(2,1)}), bf16[128,8,128]{2,0,1:T(8,128)(2,1)S(1)}, u32[]{:S(2)}, u32[]{:S(2)}) async-start(bf16[128,8,128]{2,0,1:T(8,128)(2,1)} %copy.16), calls=%async_computation.1 | async-start | bytes 524288 | tf_op jit(solution)/shard_map/all_to_all | solution.py:33
  15.3 1.3 slice_bitcast_fusion.11
  16.6 1.1 pad_maximum_fusion
  17.7 3.6 %all-to-all-done.1 = bf16[128,8,128]{2,0,1:T(8,128)(2,1)S(1)} async-done(((bf16[128,8,128]{2,0,1:T(8,128)(2,1)}), bf16[128,8,128]{2,0,1:T(8,128)(2,1)S(1)}, u32[]{:S(2)}, u32[]{:S(2)}) %all-to-all-start.1) | async-done | bytes 262176 | tf_op jit(solution)/shard_map/all_to_all | solution.py:33
  21.3 3.5 %all-to-all-start.2 = ((bf16[4,128,8,128]{3,2,1,0:T(8,128)(2,1)}), bf16[4,128,8,128]{3,2,1,0:T(8,128)(2,1)S(1)}, u32[]{:S(2)}, u32[]{:S(2)}) async-start(bf16[4,128,8,128]{3,2,1,0:T(8,128)(2,1)} %pad_maximum_fusion), calls=%async_computation.2 | async-start | bytes 2097152 | tf_op jit(solution)/shard_map/all_to_all | solution.py:24
  25.1 14.2 %all-to-all-done.2 = bf16[4,128,8,128]{3,2,1,0:T(8,128)(2,1)S(1)} async-done(((bf16[4,128,8,128]{3,2,1,0:T(8,128)(2,1)}), bf16[4,128,8,128]{3,2,1,0:T(8,128)(2,1)S(1)}, u32[]{:S(2)}, u32[]{:S(2)}) %all-to-all-start.2) | async-done | bytes 1048608 | tf_op jit(solution)/shard_map/all_to_all | solution.py:24
  39.5 119.6 %while.49 = (s32[]{:T(128)}, f32[2,4,512]{2,1,0:T(4,128)S(1)}, f32[2,4,512]{2,1,0:T(4,128)S(1)}, f32[2,4,512,128]{3,2,1,0:T(8,128)}, bf16[2,512,2,128]{3,1,2,0:T...) while((s32[]{:T(128)}, f32[2,4,512]{2,1,0:T(4,128)S(1)}, ...), condition=%wide.region_5.6_spmd.clone.clone, body=%wide.region_0.5_spmd.clone.clone.sunk | while | flops 7569716736 | bytes 86422968 | solution.py:114
  39.5 2.2 %collective-permute-start = (bf16[2,512,2,128]{3,1,2,0:T(8,128)(2,1)S(1)}, bf16[2,512,2,128]{3,1,2,0:T(8,128)(2,1)S(1)}, u32[]{:S(2)}, u32[]{:S(2)}) collective-permute-start(bf16[2,512,2,128]{3,1,2,0:T(8,128)(2,1)S(1)} %copy.46), channel_id=1, source_target_pairs={{0,4},{4,0},{1,5},{5,1},{2,6},{6,2},{3,7},{7,3},{8,12},{12,8},{9,1... | collective-permute-start | bytes 1572872 | tf_op jit(solution)/shard_map/while/body/eval_jaxpr/while/body/eval_jaxpr/ppermute | solution.py:18
  41.7 1.6 collective-permute-start.1
  43.8 1.5 fusion.113
  45.3 8.1 %collective-permute-done = bf16[2,512,2,128]{3,1,2,0:T(8,128)(2,1)S(1)} collective-permute-done((bf16[2,512,2,128]{3,1,2,0:T(8,128)(2,1)S(1)}, bf16[2,512,2,128]{3,1,2,0:T(8,128)(2,1)S(1)}, u32[]{:S(2)}, u32[]{:S(2)}) %collective-permute-start) | collective-permute-done | bytes 524320 | tf_op jit(solution)/shard_map/while/body/eval_jaxpr/while/body/eval_jaxpr/ppermute | solution.py:18
  53.4 1.5 fusion.112
  54.9 7.6 %fusion.117 = f32[2,4,512,128]{3,2,1,0:T(8,128)S(1)} fusion(f32[2,512,512,4]{2,1,3,0:T(8,128)S(1)} %get-tuple-element.744, f32[2,4,512]{2,1,0:T(4,128)S(1)} %get-tuple-element.745, pred[512,512]{0,1:T(8,128)(4,1)S(1)} %get-tuple-element.741, bf16[2,512,2,128]{3,1,2,0:T(8,128)(2,1)S(1)} %copy.46), kind=kOutput, calls=%fused_computation.11.clone.1 | convolution fusion | flops 3229614080 | bytes 11026432 | tf_op jit(solution)/shard_map/while/body/eval_jaxpr/kgts,skd->kgtd/dot_general | solution.py:66
  62.6 4.1 %fusion.115 = (f32[2,4,512]{2,1,0:T(4,128)S(1)}, f32[2,4,512]{2,1,0:T(4,128)S(1)}) fusion(f32[2,512,512,4]{2,1,3,0:T(8,128)S(1)} %get-tuple-element.744, f32[2,4,512]{2,1,0:T(4,128)S(1)} %get-tuple-element.745, pred[512,512]{0,1:T(8,128)(4,1)S(1)} %get-tuple-element.741, f32[2,4,512]{2,1,0:T(4,128)S(1)} %get-tuple-element.781, ...), kind=kLoop, calls=%fused_computation.12.clone.1 | loop fusion | flops 20963328 | bytes 17367040 | tf_op jit(solution)/shard_map/while/body/eval_jaxpr/reduce_sum | solution.py:65
  66.7 9.6 %fusion.118 = f32[2,4,512,128]{3,2,1,0:T(8,128)S(1)} fusion(f32[2,4,512,128]{3,2,1,0:T(8,128)S(1)} %fusion.117, f32[2,4,512,128]{3,2,1,0:T(8,128)S(1)} %copy-done, f32[2,512,512,4]{2,1,3,0:T(8,128)S(1)} %get-tuple-element.746, f32[2,4,512]{2,1,0:T(4,128)S(1)} %get-tuple-element.781, pred[512,512]{0,1:T(8,128)(4,1)S(1)} %get-tuple-element.739, ...), kind=kOutput, calls=%fused_computation.28.clone.1 | convolution fusion | flops 3232235520 | bytes 15253505 | tf_op jit(solution)/shard_map/while/body/eval_jaxpr/while/body/eval_jaxpr/kgts,skd->kgtd/dot_general | solution.py:66
  76.3 1.3 copy-done.1
  77.7 1.8 collective-permute-start
  79.5 1.6 collective-permute-start.1
  81.5 1.5 fusion.113
  83.0 7.5 %collective-permute-done = bf16[2,512,2,128]{3,1,2,0:T(8,128)(2,1)S(1)} collective-permute-done((bf16[2,512,2,128]{3,1,2,0:T(8,128)(2,1)S(1)}, bf16[2,512,2,128]{3,1,2,0:T(8,128)(2,1)S(1)}, u32[]{:S(2)}, u32[]{:S(2)}) %collective-permute-start) | collective-permute-done | bytes 524320 | tf_op jit(solution)/shard_map/while/body/eval_jaxpr/while/body/eval_jaxpr/ppermute | solution.py:18
  90.5 1.5 fusion.112
  92.1 7.6 %fusion.117 = f32[2,4,512,128]{3,2,1,0:T(8,128)S(1)} fusion(f32[2,512,512,4]{2,1,3,0:T(8,128)S(1)} %get-tuple-element.744, f32[2,4,512]{2,1,0:T(4,128)S(1)} %get-tuple-element.745, pred[512,512]{0,1:T(8,128)(4,1)S(1)} %get-tuple-element.741, bf16[2,512,2,128]{3,1,2,0:T(8,128)(2,1)S(1)} %copy.46), kind=kOutput, calls=%fused_computation.11.clone.1 | convolution fusion | flops 3229614080 | bytes 11026432 | tf_op jit(solution)/shard_map/while/body/eval_jaxpr/kgts,skd->kgtd/dot_general | solution.py:66
  99.7 4.1 %fusion.115 = (f32[2,4,512]{2,1,0:T(4,128)S(1)}, f32[2,4,512]{2,1,0:T(4,128)S(1)}) fusion(f32[2,512,512,4]{2,1,3,0:T(8,128)S(1)} %get-tuple-element.744, f32[2,4,512]{2,1,0:T(4,128)S(1)} %get-tuple-element.745, pred[512,512]{0,1:T(8,128)(4,1)S(1)} %get-tuple-element.741, f32[2,4,512]{2,1,0:T(4,128)S(1)} %get-tuple-element.781, ...), kind=kLoop, calls=%fused_computation.12.clone.1 | loop fusion | flops 20963328 | bytes 17367040 | tf_op jit(solution)/shard_map/while/body/eval_jaxpr/reduce_sum | solution.py:65
  103.8 9.6 %fusion.118 = f32[2,4,512,128]{3,2,1,0:T(8,128)S(1)} fusion(f32[2,4,512,128]{3,2,1,0:T(8,128)S(1)} %fusion.117, f32[2,4,512,128]{3,2,1,0:T(8,128)S(1)} %copy-done, f32[2,512,512,4]{2,1,3,0:T(8,128)S(1)} %get-tuple-element.746, f32[2,4,512]{2,1,0:T(4,128)S(1)} %get-tuple-element.781, pred[512,512]{0,1:T(8,128)(4,1)S(1)} %get-tuple-element.739, ...), kind=kOutput, calls=%fused_computation.28.clone.1 | convolution fusion | flops 3232235520 | bytes 15253505 | tf_op jit(solution)/shard_map/while/body/eval_jaxpr/while/body/eval_jaxpr/kgts,skd->kgtd/dot_general | solution.py:66
  113.4 1.3 copy-done.1
  114.8 1.5 collective-permute-start
  116.3 1.6 collective-permute-start.1
  118.3 1.5 fusion.113
  119.9 6.9 %collective-permute-done = bf16[2,512,2,128]{3,1,2,0:T(8,128)(2,1)S(1)} collective-permute-done((bf16[2,512,2,128]{3,1,2,0:T(8,128)(2,1)S(1)}, bf16[2,512,2,128]{3,1,2,0:T(8,128)(2,1)S(1)}, u32[]{:S(2)}, u32[]{:S(2)}) %collective-permute-start) | collective-permute-done | bytes 524320 | tf_op jit(solution)/shard_map/while/body/eval_jaxpr/while/body/eval_jaxpr/ppermute | solution.py:18
  126.8 1.5 fusion.112
  128.4 7.6 %fusion.117 = f32[2,4,512,128]{3,2,1,0:T(8,128)S(1)} fusion(f32[2,512,512,4]{2,1,3,0:T(8,128)S(1)} %get-tuple-element.744, f32[2,4,512]{2,1,0:T(4,128)S(1)} %get-tuple-element.745, pred[512,512]{0,1:T(8,128)(4,1)S(1)} %get-tuple-element.741, bf16[2,512,2,128]{3,1,2,0:T(8,128)(2,1)S(1)} %copy.46), kind=kOutput, calls=%fused_computation.11.clone.1 | convolution fusion | flops 3229614080 | bytes 11026432 | tf_op jit(solution)/shard_map/while/body/eval_jaxpr/kgts,skd->kgtd/dot_general | solution.py:66
  136.0 4.1 %fusion.115 = (f32[2,4,512]{2,1,0:T(4,128)S(1)}, f32[2,4,512]{2,1,0:T(4,128)S(1)}) fusion(f32[2,512,512,4]{2,1,3,0:T(8,128)S(1)} %get-tuple-element.744, f32[2,4,512]{2,1,0:T(4,128)S(1)} %get-tuple-element.745, pred[512,512]{0,1:T(8,128)(4,1)S(1)} %get-tuple-element.741, f32[2,4,512]{2,1,0:T(4,128)S(1)} %get-tuple-element.781, ...), kind=kLoop, calls=%fused_computation.12.clone.1 | loop fusion | flops 20963328 | bytes 17367040 | tf_op jit(solution)/shard_map/while/body/eval_jaxpr/reduce_sum | solution.py:65
  140.1 9.6 %fusion.118 = f32[2,4,512,128]{3,2,1,0:T(8,128)S(1)} fusion(f32[2,4,512,128]{3,2,1,0:T(8,128)S(1)} %fusion.117, f32[2,4,512,128]{3,2,1,0:T(8,128)S(1)} %copy-done, f32[2,512,512,4]{2,1,3,0:T(8,128)S(1)} %get-tuple-element.746, f32[2,4,512]{2,1,0:T(4,128)S(1)} %get-tuple-element.781, pred[512,512]{0,1:T(8,128)(4,1)S(1)} %get-tuple-element.739, ...), kind=kOutput, calls=%fused_computation.28.clone.1 | convolution fusion | flops 3232235520 | bytes 15253505 | tf_op jit(solution)/shard_map/while/body/eval_jaxpr/while/body/eval_jaxpr/kgts,skd->kgtd/dot_general | solution.py:66
  149.7 1.3 copy-done.1
  159.1 1.3 collective-permute-start.2
  160.7 1.5 fusion.55
  162.2 8.0 %collective-permute-done.2 = bf16[2,512,2,128]{3,1,2,0:T(8,128)(2,1)S(1)} collective-permute-done((bf16[2,512,2,128]{3,1,2,0:T(8,128)(2,1)S(1)}, bf16[2,512,2,128]{3,1,2,0:T(8,128)(2,1)S(1)}, u32[]{:S(2)}, u32[]{:S(2)}) %collective-permute-start.2) | collective-permute-done | bytes 524320 | tf_op jit(solution)/shard_map/while/body/eval_jaxpr/ppermute | solution.py:18
  170.2 1.5 fusion.56
  171.8 7.6 %fusion.58 = f32[2,4,512,128]{3,2,1,0:T(8,128)S(1)} fusion(f32[2,512,512,4]{2,1,3,0:T(8,128)S(1)} %get-tuple-element.653, f32[2,4,512]{2,1,0:T(4,128)S(1)} %bitcast.175, pred[512,512]{0,1:T(8,128)(4,1)S(1)} %get-tuple-element.648, bf16[2,512,2,128]{3,1,2,0:T(8,128)(2,1)S(1)} %get-tuple-element.515), kind=kOutput, calls=%fused_computation.78 | convolution fusion | flops 3229614080 | bytes 11026432 | tf_op jit(solution)/shard_map/kgts,skd->kgtd/dot_general | solution.py:66
  179.4 4.2 %fusion.57 = (f32[2,4,512]{2,1,0:T(4,128)S(1)}, f32[2,4,512]{2,1,0:T(4,128)S(1)}) fusion(f32[2,512,512,4]{2,1,3,0:T(8,128)S(1)} %get-tuple-element.653, f32[2,4,512]{2,1,0:T(4,128)S(1)} %bitcast.176, pred[512,512]{0,1:T(8,128)(4,1)S(1)} %get-tuple-element.648, f32[2,4,512]{2,1,0:T(4,128)S(1)} %bitcast.173, f32[2,512,512,4]{2,1,3,0:T(8,128)S(1)} %get-tuple-element.651, ...), kind=kLoop, calls=%fused_computation.77 | loop fusion | flops 20963328 | bytes 17367040 | tf_op jit(solution)/shard_map/reduce_sum | solution.py:65
  183.6 9.4 %divide_convert_fusion = bf16[2,4,512,128]{3,2,1,0:T(8,128)(2,1)S(1)} fusion(f32[2,4,512,128]{3,2,1,0:T(8,128)S(1)} %fusion.58, f32[2,4,512,128]{3,2,1,0:T(8,128)S(1)} %copy-done.2, f32[2,512,512,4]{2,1,3,0:T(8,128)S(1)} %get-tuple-element.651, f32[2,4,512]{2,1,0:T(4,128)S(1)} %bitcast.174, pred[512,512]{0,1:T(8,128)(4,1)S(1)} %get-tuple-element.649, ...), kind=kOutput, calls=%fused_computation.91 | convolution fusion | flops 3232759808 | bytes 14221312 | tf_op jit(solution)/shard_map/while/body/eval_jaxpr/kgts,skd->kgtd/dot_general | solution.py:66
  193.0 0.7 copy.21
  193.7 17.4 %all_to_all.53 = bf16[512,8,128]{2,1,0:T(8,128)(2,1)S(1)} all-to-all(bf16[512,8,128]{2,1,0:T(8,128)(2,1)S(1)} %copy.21), channel_id=1, replica_groups=mesh['head'=4,'inner'=2,'outer'=4] {'head'}, dimensions={0} | all-to-all | bytes 2097152 | tf_op jit(solution)/shard_map/all_to_all | solution.py:119
  211.1 1.1 copy.36
  (51 shorter events, 2.3 us)
Async XLA Ops:
  1.7 10.2 %all-to-all-start = ((bf16[128,8,128]{2,0,1:T(8,128)(2,1)}), bf16[128,8,128]{2,0,1:T(8,128)(2,1)S(1)}, u32[]{:S(2)}, u32[]{:S(2)}) async-start(bf16[128,8,128]{2,0,1:T(8,128)(2,1)} %copy.14), calls=%async_computation | async-start | bytes 524288 | tf_op jit(solution)/shard_map/all_to_all | solution.py:32
  11.9 9.4 %all-to-all-start.1 = ((bf16[128,8,128]{2,0,1:T(8,128)(2,1)}), bf16[128,8,128]{2,0,1:T(8,128)(2,1)S(1)}, u32[]{:S(2)}, u32[]{:S(2)}) async-start(bf16[128,8,128]{2,0,1:T(8,128)(2,1)} %copy.16), calls=%async_computation.1 | async-start | bytes 524288 | tf_op jit(solution)/shard_map/all_to_all | solution.py:33
  21.3 17.9 %all-to-all-start.2 = ((bf16[4,128,8,128]{3,2,1,0:T(8,128)(2,1)}), bf16[4,128,8,128]{3,2,1,0:T(8,128)(2,1)S(1)}, u32[]{:S(2)}, u32[]{:S(2)}) async-start(bf16[4,128,8,128]{3,2,1,0:T(8,128)(2,1)} %pad_maximum_fusion), calls=%async_computation.2 | async-start | bytes 2097152 | tf_op jit(solution)/shard_map/all_to_all | solution.py:24
  39.5 13.8 %collective-permute-start = (bf16[2,512,2,128]{3,1,2,0:T(8,128)(2,1)S(1)}, bf16[2,512,2,128]{3,1,2,0:T(8,128)(2,1)S(1)}, u32[]{:S(2)}, u32[]{:S(2)}) collective-permute-start(bf16[2,512,2,128]{3,1,2,0:T(8,128)(2,1)S(1)} %copy.46), channel_id=1, source_target_pairs={{0,4},{4,0},{1,5},{5,1},{2,6},{6,2},{3,7},{7,3},{8,12},{12,8},{9,1... | collective-permute-start | bytes 1572872 | tf_op jit(solution)/shard_map/while/body/eval_jaxpr/while/body/eval_jaxpr/ppermute | solution.py:18
  41.7 34.5 %collective-permute-start.1 = (bf16[2,512,2,128]{3,1,2,0:T(8,128)(2,1)S(1)}, bf16[2,512,2,128]{3,1,2,0:T(8,128)(2,1)S(1)}, u32[]{:S(2)}, u32[]{:S(2)}) collective-permute-start(bf16[2,512,2,128]{3,1,2,0:T(8,128)(2,1)S(1)} %copy.46), channel_id=1, source_target_pairs={{0,1},{1,2},{2,3},{3,0},{4,5},{5,6},{6,7},{7,4},{8,9},{9,10},{10,1... | collective-permute-start | bytes 1572872 | tf_op jit(solution)/shard_map/while/body/eval_jaxpr/ppermute | solution.py:18
  62.6 4.1 %copy-start = (f32[2,4,512,128]{3,2,1,0:T(8,128)S(1)}, f32[2,4,512,128]{3,2,1,0:T(8,128)}, u32[]{:S(2)}) copy-start(f32[2,4,512,128]{3,2,1,0:T(8,128)} %get-tuple-element.769) | copy-start | bytes 6291460 | tf_op jit(solution)/shard_map/while
  76.3 1.3 copy-start.1
  77.7 12.9 %collective-permute-start = (bf16[2,512,2,128]{3,1,2,0:T(8,128)(2,1)S(1)}, bf16[2,512,2,128]{3,1,2,0:T(8,128)(2,1)S(1)}, u32[]{:S(2)}, u32[]{:S(2)}) collective-permute-start(bf16[2,512,2,128]{3,1,2,0:T(8,128)(2,1)S(1)} %copy.46), channel_id=1, source_target_pairs={{0,4},{4,0},{1,5},{5,1},{2,6},{6,2},{3,7},{7,3},{8,12},{12,8},{9,1... | collective-permute-start | bytes 1572872 | tf_op jit(solution)/shard_map/while/body/eval_jaxpr/while/body/eval_jaxpr/ppermute | solution.py:18
  79.5 34.0 %collective-permute-start.1 = (bf16[2,512,2,128]{3,1,2,0:T(8,128)(2,1)S(1)}, bf16[2,512,2,128]{3,1,2,0:T(8,128)(2,1)S(1)}, u32[]{:S(2)}, u32[]{:S(2)}) collective-permute-start(bf16[2,512,2,128]{3,1,2,0:T(8,128)(2,1)S(1)} %copy.46), channel_id=1, source_target_pairs={{0,1},{1,2},{2,3},{3,0},{4,5},{5,6},{6,7},{7,4},{8,9},{9,10},{10,1... | collective-permute-start | bytes 1572872 | tf_op jit(solution)/shard_map/while/body/eval_jaxpr/ppermute | solution.py:18
  99.7 4.1 %copy-start = (f32[2,4,512,128]{3,2,1,0:T(8,128)S(1)}, f32[2,4,512,128]{3,2,1,0:T(8,128)}, u32[]{:S(2)}) copy-start(f32[2,4,512,128]{3,2,1,0:T(8,128)} %get-tuple-element.769) | copy-start | bytes 6291460 | tf_op jit(solution)/shard_map/while
  113.4 1.3 copy-start.1
  114.8 12.0 %collective-permute-start = (bf16[2,512,2,128]{3,1,2,0:T(8,128)(2,1)S(1)}, bf16[2,512,2,128]{3,1,2,0:T(8,128)(2,1)S(1)}, u32[]{:S(2)}, u32[]{:S(2)}) collective-permute-start(bf16[2,512,2,128]{3,1,2,0:T(8,128)(2,1)S(1)} %copy.46), channel_id=1, source_target_pairs={{0,4},{4,0},{1,5},{5,1},{2,6},{6,2},{3,7},{7,3},{8,12},{12,8},{9,1... | collective-permute-start | bytes 1572872 | tf_op jit(solution)/shard_map/while/body/eval_jaxpr/while/body/eval_jaxpr/ppermute | solution.py:18
  116.3 33.4 %collective-permute-start.1 = (bf16[2,512,2,128]{3,1,2,0:T(8,128)(2,1)S(1)}, bf16[2,512,2,128]{3,1,2,0:T(8,128)(2,1)S(1)}, u32[]{:S(2)}, u32[]{:S(2)}) collective-permute-start(bf16[2,512,2,128]{3,1,2,0:T(8,128)(2,1)S(1)} %copy.46), channel_id=1, source_target_pairs={{0,1},{1,2},{2,3},{3,0},{4,5},{5,6},{6,7},{7,4},{8,9},{9,10},{10,1... | collective-permute-start | bytes 1572872 | tf_op jit(solution)/shard_map/while/body/eval_jaxpr/ppermute | solution.py:18
  136.0 4.1 %copy-start = (f32[2,4,512,128]{3,2,1,0:T(8,128)S(1)}, f32[2,4,512,128]{3,2,1,0:T(8,128)}, u32[]{:S(2)}) copy-start(f32[2,4,512,128]{3,2,1,0:T(8,128)} %get-tuple-element.769) | copy-start | bytes 6291460 | tf_op jit(solution)/shard_map/while
  149.7 1.3 copy-start.1
  159.1 11.1 %collective-permute-start.2 = (bf16[2,512,2,128]{3,1,2,0:T(8,128)(2,1)S(1)}, bf16[2,512,2,128]{3,1,2,0:T(8,128)(2,1)S(1)}, u32[]{:S(2)}, u32[]{:S(2)}) collective-permute-start(bf16[2,512,2,128]{3,1,2,0:T(8,128)(2,1)S(1)} %get-tuple-element.515), channel_id=1, source_target_pairs={{0,4},{4,0},{1,5},{5,1},{2,6},{6,2},{3,7},{7,3},{8,12},{12,8},{9,1... | collective-permute-start | bytes 1572872 | tf_op jit(solution)/shard_map/while/body/eval_jaxpr/ppermute | solution.py:18
  179.4 4.3 %copy-start.2 = (f32[2,4,512,128]{3,2,1,0:T(8,128)S(1)}, f32[2,4,512,128]{3,2,1,0:T(8,128)}, u32[]{:S(2)}) copy-start(f32[2,4,512,128]{3,2,1,0:T(8,128)} %get-tuple-element.513) | copy-start | bytes 6291460
